TPU v7x, 32 devices: a whole 2x2x4 slice. The times are simulated.
32 devices in a mesh: blk: 16 (over z, y, core), team: 2 (over x).
Axes of the slice: x: 2, y: 2, z: 4, core: 2. Of those that a mesh axis runs over, the one named last changes fastest.
Arguments:
- positions: float32 [16384, 3], P('blk'), may hold values from 0 to 1
- velocity: float32 [16384, 3], P('blk'), may hold values from -6 to 6
- masses: float32 [16384], P('blk'), may hold values from 6.1035157e-06 to 0.00061035156
Outputs:
- accel: float32 [16384, 3], P('blk')
- velocity_next: float32 [16384, 3], P('blk')
- positions_next: float32 [16384, 3], P('blk')
All inputs are finite; a program needn't handle non-finite values.
Results may differ from a plain program's by a relative error of at most 0.0003.
Values sent between devices are 32-bit elements.
A program may use at most 64 MiB of HBM per device.

v0:
```python
import jax
import jax.numpy as jnp
from jax import lax
from jax.sharding import PartitionSpec as P

SOFTEN_SQ = 0.0004
TIME_STEP = 0.01


def passed_along(block, axis, distance):
    devices = range(lax.axis_size(axis))
    route = [((i - distance) % len(devices), i) for i in devices]
    return lax.ppermute(block, axis, route)


def attract(targets, sources):
    deltas = [sources[None, :, column] - targets[:, column : column + 1] for column in range(3)]
    dist_sq = deltas[0] * deltas[0] + deltas[1] * deltas[1] + deltas[2] * deltas[2] + SOFTEN_SQ
    inverse = lax.rsqrt(dist_sq)
    weight = sources[None, :, 3] * inverse * inverse * inverse
    return jnp.stack([jnp.sum(weight * delta, axis=1) for delta in deltas], axis=1)


def per_device(positions, velocity, masses):
    packed = jnp.concatenate([positions, masses[:, None]], axis=1)
    blocks = lax.axis_size("blk")
    half = blocks // 2
    member = lax.axis_index("team")
    rows = positions.shape[0]
    following = passed_along(packed, "blk", -1)
    doubled = jnp.concatenate([packed, following], axis=0)
    far = passed_along(doubled, "blk", -half)
    carried = jnp.where(member == 1, far, doubled)

    def advance_pair(counter, state):
        summed, holding = state
        summed = summed + attract(positions, holding)
        return (summed, passed_along(holding, "blk", -2))

    summed, carried = lax.fori_loop(
        0, half // 2 - 1, advance_pair, (jnp.zeros((rows, 3), jnp.float32), carried)
    )
    summed = summed + attract(positions, carried)
    accel = lax.psum(summed, "team")
    velocity_next = velocity + TIME_STEP * accel
    positions_next = positions + TIME_STEP * velocity_next
    return (accel, velocity_next, positions_next)


def solution(mesh):
    in_specs = (P("blk", None), P("blk", None), P("blk"))
    out_specs = (P("blk", None), P("blk", None), P("blk", None))
    return jax.shard_map(
        per_device, mesh=mesh, in_specs=in_specs, out_specs=out_specs, check_vma=False
    )
```

profile of v0, /device:TPU:0, one launch (start us, length us, event | category | flops | bytes accessed | tf_op | source)
XLA Modules:
  0.0 52.1 jit_solution(14040459949676174283)
XLA Ops:
  0.6 0.0 copy-start.2
  0.6 0.0 copy-start
  0.6 0.8 %pad_maximum_fusion.1 = f32[1024,4]{0,1:T(4,128)S(1)} fusion(f32[1024,1]{0,1:T(1,128)} %bitcast.51, f32[1024,3]{0,1:T(4,128)} %param.5), kind=kLoop, calls=%fused_computation.30 | loop fusion | flops 4096 | bytes 32768 | tf_op jit(solution)/shard_map/concatenate | solution.py:25
  1.4 5.5 %collective-permute-start.1 = (f32[1024,4]{0,1:T(4,128)S(1)}, f32[1024,4]{0,1:T(4,128)S(1)}, u32[]{:S(2)}, u32[]{:S(2)}) collective-permute-start(f32[1024,4]{0,1:T(4,128)S(1)} %pad_maximum_fusion.1), channel_id=1, source_target_pairs={{2,0},{4,2},{6,4},{8,6},{10,8},{12,10},{14,12},{16,14},{18,16},{20... | collective-permute-start | bytes 49160 | tf_op jit(solution)/shard_map/ppermute | solution.py:13
  7.0 1.4 %collective-permute-done.1 = f32[1024,4]{0,1:T(4,128)S(1)} collective-permute-done((f32[1024,4]{0,1:T(4,128)S(1)}, f32[1024,4]{0,1:T(4,128)S(1)}, u32[]{:S(2)}, u32[]{:S(2)}) %collective-permute-start.1) | collective-permute-done | bytes 16416 | tf_op jit(solution)/shard_map/ppermute | solution.py:13
  8.4 0.0 copy-done.2
  8.4 0.0 copy-done
  8.4 0.1 collective-permute-start.2
  8.6 4.8 %collective-permute-done.2 = f32[2048,4]{0,1:T(4,128)S(1)} collective-permute-done((f32[2048,4]{0,1:T(4,128)S(1)}, f32[2048,4]{0,1:T(4,128)S(1)}, u32[]{:S(2)}, u32[]{:S(2)}) %collective-permute-start.2) | collective-permute-done | bytes 32800 | tf_op jit(solution)/shard_map/ppermute | solution.py:13
  13.3 23.2 %while.13 = (s32[]{:T(128)}, f32[1024,3]{0,1:T(4,128)S(1)}, f32[2048,4]{0,1:T(4,128)S(1)}, f32[1024,3]{0,1:T(4,128)S(1)}, s32[]{:T(128)}, /*index=5*/s32[]{:T(128)}) while((s32[]{:T(128)}, f32[1024,3]{0,1:T(4,128)S(1)}, f32[2048,4]{0,1:T(4,128)S(1)}, f32[1024,3]{0,1:T(4,128)S(1)}, s32[]{:T(128)}, /*index=5*/s32[]{:T(128)}) %tuple.50), condition=%wide.region_4.5_spmd.clone, body=%wide.region_0.4_spmd.clone.sunk | while | flops 37757952 | bytes 381047 | solution.py:40
  13.4 0.9 %collective-permute-start = (f32[2048,4]{0,1:T(4,128)S(1)}, f32[2048,4]{0,1:T(4,128)S(1)}, u32[]{:S(2)}, u32[]{:S(2)}) collective-permute-start(f32[2048,4]{0,1:T(4,128)S(1)} %copy.11), channel_id=1, source_target_pairs={{4,0},{6,2},{8,4},{10,6},{12,8},{14,10},{16,12},{18,14},{20,16},{2... | collective-permute-start | bytes 98312 | tf_op jit(solution)/shard_map/while/body/eval_jaxpr/ppermute | solution.py:13
  14.3 6.7 %fusion.23 = (f32[1024]{0:T(1024)S(1)}, f32[1024]{0:T(1024)S(1)}, f32[1024]{0:T(1024)S(1)}) fusion(f32[1024]{0:T(1024)S(1)} %bitcast.50, f32[2048]{0:T(1024)S(1)} %bitcast.44, f32[1024]{0:T(1024)S(1)} %bitcast.49, f32[2048]{0:T(1024)S(1)} %bitcast.42, f32[1024]{0:T(1024)S(1)} %bitcast.48, f32[2048]{0:T(1024)S(1)} %bitcast.43, f32[2048]{0:T(1024)S(1)} %bitcast.41), kind=kLoop, calls=%fused_computation.11.clone.1 | loop fusion | flops 37745664 | bytes 57344 | tf_op jit(solution)/shard_map/while/body/eval_jaxpr/reduce_sum | solution.py:21
  21.0 0.0 collective-permute-done
  21.0 1.9 %collective-permute-start = (f32[2048,4]{0,1:T(4,128)S(1)}, f32[2048,4]{0,1:T(4,128)S(1)}, u32[]{:S(2)}, u32[]{:S(2)}) collective-permute-start(f32[2048,4]{0,1:T(4,128)S(1)} %copy.11), channel_id=1, source_target_pairs={{4,0},{6,2},{8,4},{10,6},{12,8},{14,10},{16,12},{18,14},{20,16},{2... | collective-permute-start | bytes 98312 | tf_op jit(solution)/shard_map/while/body/eval_jaxpr/ppermute | solution.py:13
  22.9 6.7 %fusion.23 = (f32[1024]{0:T(1024)S(1)}, f32[1024]{0:T(1024)S(1)}, f32[1024]{0:T(1024)S(1)}) fusion(f32[1024]{0:T(1024)S(1)} %bitcast.50, f32[2048]{0:T(1024)S(1)} %bitcast.44, f32[1024]{0:T(1024)S(1)} %bitcast.49, f32[2048]{0:T(1024)S(1)} %bitcast.42, f32[1024]{0:T(1024)S(1)} %bitcast.48, f32[2048]{0:T(1024)S(1)} %bitcast.43, f32[2048]{0:T(1024)S(1)} %bitcast.41), kind=kLoop, calls=%fused_computation.11.clone.1 | loop fusion | flops 37745664 | bytes 57344 | tf_op jit(solution)/shard_map/while/body/eval_jaxpr/reduce_sum | solution.py:21
  29.6 0.0 collective-permute-done
  29.7 0.1 collective-permute-start
  29.8 6.7 %fusion.23 = (f32[1024]{0:T(1024)S(1)}, f32[1024]{0:T(1024)S(1)}, f32[1024]{0:T(1024)S(1)}) fusion(f32[1024]{0:T(1024)S(1)} %bitcast.50, f32[2048]{0:T(1024)S(1)} %bitcast.44, f32[1024]{0:T(1024)S(1)} %bitcast.49, f32[2048]{0:T(1024)S(1)} %bitcast.42, f32[1024]{0:T(1024)S(1)} %bitcast.48, f32[2048]{0:T(1024)S(1)} %bitcast.43, f32[2048]{0:T(1024)S(1)} %bitcast.41), kind=kLoop, calls=%fused_computation.11.clone.1 | loop fusion | flops 37745664 | bytes 57344 | tf_op jit(solution)/shard_map/while/body/eval_jaxpr/reduce_sum | solution.py:21
  36.5 0.0 collective-permute-done
  36.6 6.7 %fusion.11 = (f32[1024]{0:T(1024)S(1)}, f32[1024]{0:T(1024)S(1)}, f32[1024]{0:T(1024)S(1)}) fusion(f32[1024]{0:T(1024)S(1)} %bitcast.59, f32[2048]{0:T(1024)S(1)} %bitcast.55, f32[1024]{0:T(1024)S(1)} %bitcast.60, f32[2048]{0:T(1024)S(1)} %bitcast.56, f32[1024]{0:T(1024)S(1)} %bitcast.58, f32[2048]{0:T(1024)S(1)} %bitcast.57, f32[2048]{0:T(1024)S(1)} %bitcast.54), kind=kLoop, calls=%fused_computation.26 | loop fusion | flops 37745664 | bytes 57344 | tf_op jit(solution)/shard_map/reduce_sum | solution.py:21
  43.2 0.0 copy-start.3
  43.3 8.1 %psum.7 = f32[1024,3]{0,1:T(4,128)S(1)} all-reduce(f32[1024,3]{0,1:T(4,128)S(1)} %maximum_add_fusion.1), channel_id=1, replica_groups=mesh['blk'=16,'team'=2] {'team'}, use_global_device_ids=true, to_apply=%region_8.9 | all-reduce | flops 3072 | bytes 24576 | tf_op jit(solution)/shard_map/psum | solution.py:44
  51.4 0.0 copy-done.3
  51.4 0.0 copy-start.1
  51.4 0.6 %multiply_add_fusion = (f32[1024,3]{0,1:T(4,128)}, f32[1024,3]{0,1:T(4,128)}) fusion(f32[1024,3]{0,1:T(4,128)S(1)} %get-tuple-element.138, f32[1024,3]{0,1:T(4,128)S(1)} %copy-done.3, f32[1024,3]{0,1:T(4,128)S(1)} %psum.7), kind=kLoop, calls=%fused_computation.32 | loop fusion | flops 12288 | bytes 61440 | tf_op jit(solution)/shard_map/add | solution.py:46
  52.1 0.0 copy-done.1
  (18 shorter events, 0.3 us)
Async XLA Ops:
  0.6 7.8 %copy-start.2 = (f32[1024]{0:T(1024)S(1)}, f32[1024]{0:T(1024)}, u32[]{:S(2)}) copy-start(f32[1024]{0:T(1024)} %param.7) | copy-start | bytes 12292
  0.6 7.8 %copy-start = (f32[1024,3]{0,1:T(4,128)S(1)}, f32[1024,3]{0,1:T(4,128)}, u32[]{:S(2)}) copy-start(f32[1024,3]{0,1:T(4,128)} %param.5) | copy-start | bytes 36868
  1.4 7.0 %collective-permute-start.1 = (f32[1024,4]{0,1:T(4,128)S(1)}, f32[1024,4]{0,1:T(4,128)S(1)}, u32[]{:S(2)}, u32[]{:S(2)}) collective-permute-start(f32[1024,4]{0,1:T(4,128)S(1)} %pad_maximum_fusion.1), channel_id=1, source_target_pairs={{2,0},{4,2},{6,4},{8,6},{10,8},{12,10},{14,12},{16,14},{18,16},{20... | collective-permute-start | bytes 49160 | tf_op jit(solution)/shard_map/ppermute | solution.py:13
  8.4 4.9 %collective-permute-start.2 = (f32[2048,4]{0,1:T(4,128)S(1)}, f32[2048,4]{0,1:T(4,128)S(1)}, u32[]{:S(2)}, u32[]{:S(2)}) collective-permute-start(f32[2048,4]{0,1:T(4,128)S(1)} %pad_maximum_fusion), channel_id=1, source_target_pairs={{16,0},{18,2},{20,4},{22,6},{24,8},{26,10},{28,12},{30,14},{0,16},... | collective-permute-start | bytes 98312 | tf_op jit(solution)/shard_map/ppermute | solution.py:13
  13.4 7.6 %collective-permute-start = (f32[2048,4]{0,1:T(4,128)S(1)}, f32[2048,4]{0,1:T(4,128)S(1)}, u32[]{:S(2)}, u32[]{:S(2)}) collective-permute-start(f32[2048,4]{0,1:T(4,128)S(1)} %copy.11), channel_id=1, source_target_pairs={{4,0},{6,2},{8,4},{10,6},{12,8},{14,10},{16,12},{18,14},{20,16},{2... | collective-permute-start | bytes 98312 | tf_op jit(solution)/shard_map/while/body/eval_jaxpr/ppermute | solution.py:13
  21.0 8.6 %collective-permute-start = (f32[2048,4]{0,1:T(4,128)S(1)}, f32[2048,4]{0,1:T(4,128)S(1)}, u32[]{:S(2)}, u32[]{:S(2)}) collective-permute-start(f32[2048,4]{0,1:T(4,128)S(1)} %copy.11), channel_id=1, source_target_pairs={{4,0},{6,2},{8,4},{10,6},{12,8},{14,10},{16,12},{18,14},{20,16},{2... | collective-permute-start | bytes 98312 | tf_op jit(solution)/shard_map/while/body/eval_jaxpr/ppermute | solution.py:13
  29.7 6.9 %collective-permute-start = (f32[2048,4]{0,1:T(4,128)S(1)}, f32[2048,4]{0,1:T(4,128)S(1)}, u32[]{:S(2)}, u32[]{:S(2)}) collective-permute-start(f32[2048,4]{0,1:T(4,128)S(1)} %copy.11), channel_id=1, source_target_pairs={{4,0},{6,2},{8,4},{10,6},{12,8},{14,10},{16,12},{18,14},{20,16},{2... | collective-permute-start | bytes 98312 | tf_op jit(solution)/shard_map/while/body/eval_jaxpr/ppermute | solution.py:13
  43.2 8.2 %copy-start.3 = (f32[1024,3]{0,1:T(4,128)S(1)}, f32[1024,3]{0,1:T(4,128)}, u32[]{:S(2)}) copy-start(f32[1024,3]{0,1:T(4,128)} %param.6) | copy-start | bytes 36868
  51.4 0.6 %copy-start.1 = (f32[1024,3]{0,1:T(4,128)}, f32[1024,3]{0,1:T(4,128)S(1)}, u32[]{:S(2)}) copy-start(f32[1024,3]{0,1:T(4,128)S(1)} %psum.7) | copy-start | bytes 36868
where the time goes:
time: 52.3 us; the launch traced here: 52.1 us
  other arithmetic  28.2 us (54%)
  starting transfers between devices  8.48 us (16%)
  blocking collectives  8.15 us (16%)
  waiting for transfers between devices  6.22 us (12%)
  between operations  0.73 us (1%)
    reduce_sum x4, other arithmetic, attract(): jnp.sum(weight * delta, axis=1)  26.6 us
    ppermute x5, starting transfers between devices, passed_along(): return lax.ppermute(block, axis, route)  8.48 us
    psum x1, blocking collectives, per_device(): accel = lax.psum(summed, 'team')  8.15 us
    ppermute x5, waiting for transfers between devices, passed_along(): return lax.ppermute(block, axis, route)  6.22 us
  transfers between devices with their start and end apart: 5, of which 2 were waited for; matrix products, arithmetic and copies ran while one was open for 39% of the time, Pallas kernels for 0%

commit v1 on v0

--- a/solution.py
+++ b/solution.py
@@ -41,7 +41,8 @@
         0, half // 2 - 1, advance_pair, (jnp.zeros((rows, 3), jnp.float32), carried)
     )
     summed = summed + attract(positions, carried)
-    accel = lax.psum(summed, "team")
+    parts = lax.all_gather(summed, "team")
+    accel = jnp.sum(parts, axis=0)
     velocity_next = velocity + TIME_STEP * accel
     positions_next = positions + TIME_STEP * velocity_next
     return (accel, velocity_next, positions_next)

time: 52.3 us -> 49.4 us (0.945)
  blocking collectives: 8.15 us -> 4.41 us
  local copies, waits for them, and re-layouts: 0.17 us -> 0.87 us
    psum x1 -> x0, blocking collectives: 8.15 us -> none  [per_device(): accel = lax.psum(summed, 'team')]
    all_gather x0 -> x1, blocking collectives: none -> 4.41 us  [per_device(): parts = lax.all_gather(summed, 'team')]
    unnamed x8, local copies, waits for them, and re-layouts: 0.02 us -> 0.68 us
  transfers between devices with their start and end apart: 5 -> 5, of which waited for: 2 -> 2; matrix products, arithmetic and copies ran while one was open for 39% -> 41% of each run, Pallas kernels for 0% -> 0%
where the time goes in v1:
time: 49.4 us; the launch traced here: 49.1 us
  other arithmetic  28.2 us (57%)
  starting transfers between devices  8.48 us (17%)
  waiting for transfers between devices  6.22 us (13%)
  blocking collectives  4.41 us (9%)
  local copies, waits for them, and re-layouts  0.87 us (2%)
  between operations  0.73 us (1%)
    reduce_sum x4, other arithmetic, attract(): jnp.sum(weight * delta, axis=1)  26.6 us
    ppermute x5, starting transfers between devices, passed_along(): return lax.ppermute(block, axis, route)  8.48 us
    ppermute x5, waiting for transfers between devices, passed_along(): return lax.ppermute(block, axis, route)  6.22 us
    all_gather x1, blocking collectives, per_device(): parts = lax.all_gather(summed, 'team')  4.41 us
  transfers between devices with their start and end apart: 5, of which 2 were waited for; matrix products, arithmetic and copies ran while one was open for 41% of the time, Pallas kernels for 0%

profile of v1, /device:TPU:0, one launch (start us, length us, event | category | flops | bytes accessed | tf_op | source)
XLA Modules:
  0.0 49.1 jit_solution(1359402330956037544)
XLA Ops:
  0.6 0.0 copy-start.2
  0.6 0.0 copy-start
  0.6 0.8 %pad_maximum_fusion.1 = f32[1024,4]{0,1:T(4,128)S(1)} fusion(f32[1024,1]{0,1:T(1,128)} %bitcast.53, f32[1024,3]{0,1:T(4,128)} %param.5), kind=kLoop, calls=%fused_computation.30 | loop fusion | flops 4096 | bytes 32768 | tf_op jit(solution)/shard_map/concatenate | solution.py:25
  1.4 5.5 %collective-permute-start.1 = (f32[1024,4]{0,1:T(4,128)S(1)}, f32[1024,4]{0,1:T(4,128)S(1)}, u32[]{:S(2)}, u32[]{:S(2)}) collective-permute-start(f32[1024,4]{0,1:T(4,128)S(1)} %pad_maximum_fusion.1), channel_id=1, source_target_pairs={{2,0},{4,2},{6,4},{8,6},{10,8},{12,10},{14,12},{16,14},{18,16},{20... | collective-permute-start | bytes 49160 | tf_op jit(solution)/shard_map/ppermute | solution.py:13
  7.0 1.4 %collective-permute-done.1 = f32[1024,4]{0,1:T(4,128)S(1)} collective-permute-done((f32[1024,4]{0,1:T(4,128)S(1)}, f32[1024,4]{0,1:T(4,128)S(1)}, u32[]{:S(2)}, u32[]{:S(2)}) %collective-permute-start.1) | collective-permute-done | bytes 16416 | tf_op jit(solution)/shard_map/ppermute | solution.py:13
  8.4 0.0 copy-done.2
  8.4 0.0 copy-done
  8.4 0.1 collective-permute-start.2
  8.6 4.8 %collective-permute-done.2 = f32[2048,4]{0,1:T(4,128)S(1)} collective-permute-done((f32[2048,4]{0,1:T(4,128)S(1)}, f32[2048,4]{0,1:T(4,128)S(1)}, u32[]{:S(2)}, u32[]{:S(2)}) %collective-permute-start.2) | collective-permute-done | bytes 32800 | tf_op jit(solution)/shard_map/ppermute | solution.py:13
  13.3 23.2 %while.13 = (s32[]{:T(128)}, f32[1024,3]{0,1:T(4,128)S(1)}, f32[2048,4]{0,1:T(4,128)S(1)}, f32[1024,3]{0,1:T(4,128)S(1)}, s32[]{:T(128)}, /*index=5*/s32[]{:T(128)}) while((s32[]{:T(128)}, f32[1024,3]{0,1:T(4,128)S(1)}, f32[2048,4]{0,1:T(4,128)S(1)}, f32[1024,3]{0,1:T(4,128)S(1)}, s32[]{:T(128)}, /*index=5*/s32[]{:T(128)}) %tuple.50), condition=%wide.region_4.5_spmd.clone, body=%wide.region_0.4_spmd.clone.sunk | while | flops 37757952 | bytes 381047 | solution.py:40
  13.4 0.9 %collective-permute-start = (f32[2048,4]{0,1:T(4,128)S(1)}, f32[2048,4]{0,1:T(4,128)S(1)}, u32[]{:S(2)}, u32[]{:S(2)}) collective-permute-start(f32[2048,4]{0,1:T(4,128)S(1)} %copy.11), channel_id=1, source_target_pairs={{4,0},{6,2},{8,4},{10,6},{12,8},{14,10},{16,12},{18,14},{20,16},{2... | collective-permute-start | bytes 98312 | tf_op jit(solution)/shard_map/while/body/eval_jaxpr/ppermute | solution.py:13
  14.3 6.7 %fusion.23 = (f32[1024]{0:T(1024)S(1)}, f32[1024]{0:T(1024)S(1)}, f32[1024]{0:T(1024)S(1)}) fusion(f32[1024]{0:T(1024)S(1)} %bitcast.52, f32[2048]{0:T(1024)S(1)} %bitcast.46, f32[1024]{0:T(1024)S(1)} %bitcast.51, f32[2048]{0:T(1024)S(1)} %bitcast.44, f32[1024]{0:T(1024)S(1)} %bitcast.50, f32[2048]{0:T(1024)S(1)} %bitcast.45, f32[2048]{0:T(1024)S(1)} %bitcast.43), kind=kLoop, calls=%fused_computation.11.clone.1 | loop fusion | flops 37745664 | bytes 57344 | tf_op jit(solution)/shard_map/while/body/eval_jaxpr/reduce_sum | solution.py:21
  21.0 0.0 collective-permute-done
  21.0 1.9 %collective-permute-start = (f32[2048,4]{0,1:T(4,128)S(1)}, f32[2048,4]{0,1:T(4,128)S(1)}, u32[]{:S(2)}, u32[]{:S(2)}) collective-permute-start(f32[2048,4]{0,1:T(4,128)S(1)} %copy.11), channel_id=1, source_target_pairs={{4,0},{6,2},{8,4},{10,6},{12,8},{14,10},{16,12},{18,14},{20,16},{2... | collective-permute-start | bytes 98312 | tf_op jit(solution)/shard_map/while/body/eval_jaxpr/ppermute | solution.py:13
  22.9 6.7 %fusion.23 = (f32[1024]{0:T(1024)S(1)}, f32[1024]{0:T(1024)S(1)}, f32[1024]{0:T(1024)S(1)}) fusion(f32[1024]{0:T(1024)S(1)} %bitcast.52, f32[2048]{0:T(1024)S(1)} %bitcast.46, f32[1024]{0:T(1024)S(1)} %bitcast.51, f32[2048]{0:T(1024)S(1)} %bitcast.44, f32[1024]{0:T(1024)S(1)} %bitcast.50, f32[2048]{0:T(1024)S(1)} %bitcast.45, f32[2048]{0:T(1024)S(1)} %bitcast.43), kind=kLoop, calls=%fused_computation.11.clone.1 | loop fusion | flops 37745664 | bytes 57344 | tf_op jit(solution)/shard_map/while/body/eval_jaxpr/reduce_sum | solution.py:21
  29.6 0.0 collective-permute-done
  29.7 0.1 collective-permute-start
  29.8 6.7 %fusion.23 = (f32[1024]{0:T(1024)S(1)}, f32[1024]{0:T(1024)S(1)}, f32[1024]{0:T(1024)S(1)}) fusion(f32[1024]{0:T(1024)S(1)} %bitcast.52, f32[2048]{0:T(1024)S(1)} %bitcast.46, f32[1024]{0:T(1024)S(1)} %bitcast.51, f32[2048]{0:T(1024)S(1)} %bitcast.44, f32[1024]{0:T(1024)S(1)} %bitcast.50, f32[2048]{0:T(1024)S(1)} %bitcast.45, f32[2048]{0:T(1024)S(1)} %bitcast.43), kind=kLoop, calls=%fused_computation.11.clone.1 | loop fusion | flops 37745664 | bytes 57344 | tf_op jit(solution)/shard_map/while/body/eval_jaxpr/reduce_sum | solution.py:21
  36.5 0.0 collective-permute-done
  36.6 6.7 %fusion.11 = (f32[1024]{0:T(1024)S(1)}, f32[1024]{0:T(1024)S(1)}, f32[1024]{0:T(1024)S(1)}) fusion(f32[1024]{0:T(1024)S(1)} %bitcast.61, f32[2048]{0:T(1024)S(1)} %bitcast.57, f32[1024]{0:T(1024)S(1)} %bitcast.62, f32[2048]{0:T(1024)S(1)} %bitcast.58, f32[1024]{0:T(1024)S(1)} %bitcast.60, f32[2048]{0:T(1024)S(1)} %bitcast.59, f32[2048]{0:T(1024)S(1)} %bitcast.56), kind=kLoop, calls=%fused_computation.26 | loop fusion | flops 37745664 | bytes 57344 | tf_op jit(solution)/shard_map/reduce_sum | solution.py:21
  43.3 4.4 %all-gather = f32[2048,3]{0,1:T(4,128)S(1)} all-gather(f32[1024,3]{0,1:T(4,128)S(1)} %maximum_add_fusion.1), channel_id=2, replica_groups=mesh['blk'=16,'team'=2] {'team'}, dimensions={0}, use_global_device_ids=true | all-gather | bytes 36864 | tf_op jit(solution)/shard_map/all_gather | solution.py:44
  47.7 0.0 copy-start.3
  47.8 0.7 %copy-done.3 = f32[1024,3]{0,1:T(4,128)S(1)} copy-done((f32[1024,3]{0,1:T(4,128)S(1)}, f32[1024,3]{0,1:T(4,128)}, u32[]{:S(2)}) %copy-start.3) | copy-done | bytes 12312
  48.4 0.0 copy-start.1
  48.4 0.6 %multiply_add_fusion = (f32[1024,3]{0,1:T(4,128)}, f32[1024,3]{0,1:T(4,128)}) fusion(f32[1024,3]{0,1:T(4,128)S(1)} %get-tuple-element.138, f32[1024,3]{0,1:T(4,128)S(1)} %copy-done.3, f32[1024,3]{0,1:T(4,128)S(1)} %reduce_sum.66), kind=kLoop, calls=%fused_computation.32 | loop fusion | flops 12288 | bytes 61440 | tf_op jit(solution)/shard_map/add | solution.py:47
  49.1 0.0 copy-done.1
  (20 shorter events, 0.4 us)
Async XLA Ops:
  0.6 7.8 %copy-start.2 = (f32[1024]{0:T(1024)S(1)}, f32[1024]{0:T(1024)}, u32[]{:S(2)}) copy-start(f32[1024]{0:T(1024)} %param.7) | copy-start | bytes 12292
  0.6 7.8 %copy-start = (f32[1024,3]{0,1:T(4,128)S(1)}, f32[1024,3]{0,1:T(4,128)}, u32[]{:S(2)}) copy-start(f32[1024,3]{0,1:T(4,128)} %param.5) | copy-start | bytes 36868
  1.4 7.0 %collective-permute-start.1 = (f32[1024,4]{0,1:T(4,128)S(1)}, f32[1024,4]{0,1:T(4,128)S(1)}, u32[]{:S(2)}, u32[]{:S(2)}) collective-permute-start(f32[1024,4]{0,1:T(4,128)S(1)} %pad_maximum_fusion.1), channel_id=1, source_target_pairs={{2,0},{4,2},{6,4},{8,6},{10,8},{12,10},{14,12},{16,14},{18,16},{20... | collective-permute-start | bytes 49160 | tf_op jit(solution)/shard_map/ppermute | solution.py:13
  8.4 4.9 %collective-permute-start.2 = (f32[2048,4]{0,1:T(4,128)S(1)}, f32[2048,4]{0,1:T(4,128)S(1)}, u32[]{:S(2)}, u32[]{:S(2)}) collective-permute-start(f32[2048,4]{0,1:T(4,128)S(1)} %pad_maximum_fusion), channel_id=1, source_target_pairs={{16,0},{18,2},{20,4},{22,6},{24,8},{26,10},{28,12},{30,14},{0,16},... | collective-permute-start | bytes 98312 | tf_op jit(solution)/shard_map/ppermute | solution.py:13
  13.4 7.6 %collective-permute-start = (f32[2048,4]{0,1:T(4,128)S(1)}, f32[2048,4]{0,1:T(4,128)S(1)}, u32[]{:S(2)}, u32[]{:S(2)}) collective-permute-start(f32[2048,4]{0,1:T(4,128)S(1)} %copy.11), channel_id=1, source_target_pairs={{4,0},{6,2},{8,4},{10,6},{12,8},{14,10},{16,12},{18,14},{20,16},{2... | collective-permute-start | bytes 98312 | tf_op jit(solution)/shard_map/while/body/eval_jaxpr/ppermute | solution.py:13
  21.0 8.6 %collective-permute-start = (f32[2048,4]{0,1:T(4,128)S(1)}, f32[2048,4]{0,1:T(4,128)S(1)}, u32[]{:S(2)}, u32[]{:S(2)}) collective-permute-start(f32[2048,4]{0,1:T(4,128)S(1)} %copy.11), channel_id=1, source_target_pairs={{4,0},{6,2},{8,4},{10,6},{12,8},{14,10},{16,12},{18,14},{20,16},{2... | collective-permute-start | bytes 98312 | tf_op jit(solution)/shard_map/while/body/eval_jaxpr/ppermute | solution.py:13
  29.7 6.9 %collective-permute-start = (f32[2048,4]{0,1:T(4,128)S(1)}, f32[2048,4]{0,1:T(4,128)S(1)}, u32[]{:S(2)}, u32[]{:S(2)}) collective-permute-start(f32[2048,4]{0,1:T(4,128)S(1)} %copy.11), channel_id=1, source_target_pairs={{4,0},{6,2},{8,4},{10,6},{12,8},{14,10},{16,12},{18,14},{20,16},{2... | collective-permute-start | bytes 98312 | tf_op jit(solution)/shard_map/while/body/eval_jaxpr/ppermute | solution.py:13
  47.7 0.7 %copy-start.3 = (f32[1024,3]{0,1:T(4,128)S(1)}, f32[1024,3]{0,1:T(4,128)}, u32[]{:S(2)}) copy-start(f32[1024,3]{0,1:T(4,128)} %param.6) | copy-start | bytes 36868
  48.4 0.6 %copy-start.1 = (f32[1024,3]{0,1:T(4,128)}, f32[1024,3]{0,1:T(4,128)S(1)}, u32[]{:S(2)}) copy-start(f32[1024,3]{0,1:T(4,128)S(1)} %reduce_sum.66) | copy-start | bytes 36868
